TPU v7x, 32 devices: a whole 2x2x4 slice. The times are simulated.
32 devices in a mesh: grp: 8 (over y, x, core), rep: 4 (over z).
Axes of the slice: x: 2, y: 2, z: 4, core: 2. Of those that a mesh axis runs over, the one named last changes fastest.
Arguments:
- momentum: bfloat16 [256, 4096], P(('grp', 'rep')), may hold values from -6 to 6
- picked: int32 [256, 32], P(('grp', 'rep')), may hold values from 0 to 4095, as said below
- owner_span_order: int32 [8], replicated, may hold values from 0 to 7, each once
Outputs:
- update: bfloat16 [8, 4096], replicated
- residual_momentum: bfloat16 [256, 4096], P(('grp', 'rep'))
Inputs may be any that keep to these rules, and one draw needn't show every extreme that they name: `picked`: the 32 numbers of a row are different. `owner_span_order`: each span stands once.
All inputs are finite; a program needn't handle non-finite values.
Results may differ from a plain program's by a relative error of at most 0.013.
Values may be sent and summed in bfloat16 or wider, within the bound.
A program may use at most 64 MiB of HBM per device.

v0:
```python
import math
import jax
import jax.numpy as jnp
from jax import lax
from jax.sharding import PartitionSpec as P

BLOCK = 64
TOPK = 32
CH_OWN = 1


def dct_cosines(points):
    freq = jnp.arange(points, dtype=jnp.float32)[:, None]
    place = jnp.arange(points, dtype=jnp.float32)[None, :]
    values = jnp.cos(jnp.pi * (2.0 * place + 1.0) * freq / (2.0 * points)) * jnp.sqrt(2.0 / points)
    values = values.at[0].multiply(jnp.sqrt(0.5))
    rounded = lax.optimization_barrier(values.astype(jnp.bfloat16))
    return rounded.astype(jnp.float32)


def forward(square_low, cosines, cos_low):
    half = jnp.einsum("cab,jb->caj", square_low, cos_low, preferred_element_type=jnp.float32)
    return jnp.einsum("ia,caj->cij", cosines, half, precision=lax.Precision.HIGHEST)


def decode(dense_matrix, cosines):
    square = dense_matrix.reshape(dense_matrix.shape[0], BLOCK, BLOCK)
    half = jnp.einsum("cij,jb->cib", square, cosines, precision=lax.Precision.HIGHEST)
    full = jnp.einsum("ia,cib->cab", cosines, half, precision=lax.Precision.HIGHEST)
    return full.reshape(dense_matrix.shape[0], BLOCK * BLOCK)


def decode_sparse(dense_low, cosines, cos_low):
    square = dense_low.reshape(dense_low.shape[0], BLOCK, BLOCK)
    half = jnp.einsum("cij,jb->cib", square, cos_low, preferred_element_type=jnp.float32)
    full = jnp.einsum("ia,cib->cab", cosines, half, precision=lax.Precision.HIGHEST)
    return full.reshape(dense_low.shape[0], BLOCK * BLOCK)


def densify(values, spots):
    entries, columns = values.shape
    per_step = math.gcd(entries, max(1, 65536 // columns))
    positions = jnp.arange(BLOCK, dtype=jnp.int32)

    def one_block(pieces):
        block_values, block_spots = pieces
        zeros = jnp.zeros_like(block_values)
        row_onehot = jnp.where(
            (block_spots // BLOCK)[:, None, :] == positions[None, :, None],
            block_values[:, None, :],
            zeros[:, None, :],
        )
        column_onehot = ((block_spots % BLOCK)[:, None, :] == positions[None, :, None]).astype(
            jnp.bfloat16
        )
        dense_matrix = jnp.einsum(
            "bcy,bzy->bcz", row_onehot, column_onehot, preferred_element_type=jnp.float32
        )
        return dense_matrix.reshape(per_step, BLOCK * BLOCK)

    stacked = lax.map(
        one_block,
        (
            values.reshape(entries // per_step, per_step, columns),
            spots.reshape(entries // per_step, per_step, columns),
        ),
    )
    return stacked.reshape(entries, BLOCK * BLOCK)


def owner_sum(received):
    values, spots = received
    return densify(values[0], spots[0])


def local(momentum, picked, owner_span_order):
    cosines = dct_cosines(BLOCK)
    cos_low = cosines.astype(jnp.bfloat16)
    owners = lax.axis_size("grp")
    span_count = momentum.shape[0]
    square_low = momentum.reshape(span_count, BLOCK, BLOCK)
    transform_coefficients = forward(square_low, cosines, cos_low).reshape(
        span_count, BLOCK * BLOCK
    )
    chosen = jnp.take_along_axis(transform_coefficients, picked, axis=1).astype(jnp.bfloat16)
    own_dense = densify(chosen, picked).astype(jnp.bfloat16)
    residual_momentum = (
        momentum.astype(jnp.float32) - decode_sparse(own_dense, cosines, cos_low)
    ).astype(jnp.bfloat16)
    slot_values = jnp.take(chosen, owner_span_order, axis=0)
    slot_spots = jnp.take(picked, owner_span_order, axis=0)
    shaped = (slot_values.reshape(owners, CH_OWN, TOPK), slot_spots.reshape(owners, CH_OWN, TOPK))
    partial_sum = owner_sum(
        (
            lax.all_to_all(shaped[0], "grp", split_axis=0, concat_axis=2, tiled=True),
            lax.all_to_all(shaped[1], "grp", split_axis=0, concat_axis=2, tiled=True),
        )
    )
    partial_sum = lax.psum(partial_sum, "rep")
    my_share = decode(partial_sum, cosines).astype(jnp.bfloat16)
    update = lax.all_gather(my_share, "grp", axis=0, tiled=True)
    return (update, residual_momentum)


def solution(mesh):
    return jax.shard_map(
        local,
        mesh=mesh,
        in_specs=(P(("grp", "rep"), None), P(("grp", "rep"), None), P()),
        out_specs=(P(), P(("grp", "rep"), None)),
        check_vma=False,
    )
```

profile of v0, /device:TPU:0, one launch (start us, length us, event | category | flops | bytes accessed | tf_op | source)
XLA Modules:
  0.0 55.1 jit_solution(13529057157685993092)
XLA Ops:
  0.6 0.0 copy-start.2
  0.6 0.7 %compare_and_fusion = pred[8]{0:T(512)(128)(4,1)S(1)} fusion(s32[8]{0:T(128)} %param.7), kind=kLoop, calls=%fused_computation.49 | loop fusion | flops 48 | bytes 40 | tf_op jit(solution)/shard_map/jit(_take)/and | solution.py:90
  1.4 0.0 copy-done.2
  1.4 0.0 copy-start
  1.4 0.0 copy-start.1
  1.4 0.6 %copy-done = s32[8,32]{1,0:T(8,128)S(1)} copy-done((s32[8,32]{1,0:T(8,128)S(1)}, s32[8,32]{1,0:T(8,128)}, u32[]{:S(2)}) %copy-start) | copy-done | bytes 1048
  2.1 0.1 reshape.340
  2.1 0.1 cosine_multiply_fusion
  2.3 0.0 copy-done.1
  2.4 0.2 reshape.317
  2.5 0.3 convolution_bitcast_fusion.2
  2.8 0.3 convolution_bitcast_fusion.1
  3.1 0.1 copy.19
  3.2 0.2 reshape.318
  3.4 2.4 %gather_fusion.2 = bf16[256]{0:T(256)(128)(2,1)S(1)} fusion(bf16[8,4096]{1,0:T(8,128)(2,1)S(1)} %reshape.318, s32[256]{0:T(256)S(1)} %reshape.340), kind=kCustom, calls=%fused_computation.2 | custom fusion | bytes 3072 | tf_op jit(solution)/shard_map/jit(take_along_axis)/gather | solution.py:85
  5.8 0.1 reshape.343
  5.9 0.6 %gather_fusion.1 = bf16[8,32]{1,0:T(8,128)(2,1)S(1)} fusion(bf16[8,32]{1,0:T(8,128)(2,1)S(1)} %select_convert_fusion, s32[1024]{0:T(1024)S(1)} %pad_clamp_fusion), kind=kCustom, calls=%fused_computation.1 | custom fusion | bytes 1056 | tf_op jit(solution)/shard_map/jit(_take)/gather | solution.py:90
  6.4 0.1 bitcast_select_fusion.1
  6.5 0.6 %copy.20 = bf16[8,1,32]{2,1,0:T(2,128)(2,1)} copy(bf16[8,1,32]{2,0,1:T(8,128)(2,1)S(1)} %bitcast_select_fusion.1) | data formatting | bytes 1024 | tf_op jit(solution)/shard_map/jit(_take)/select_n | solution.py:90
  7.1 5.2 %all-to-all-start.1 = ((bf16[8,1,32]{2,1,0:T(2,128)(2,1)}), bf16[8,1,32]{2,1,0:T(2,128)(2,1)S(1)}, u32[]{:S(2)}, u32[]{:S(2)}) async-start(bf16[8,1,32]{2,1,0:T(2,128)(2,1)} %copy.20), calls=%async_computation.1 | async-start | bytes 8192 | tf_op jit(solution)/shard_map/all_to_all | solution.py:95
  12.3 0.6 %gather_fusion = s32[8,32]{1,0:T(8,128)S(1)} fusion(s32[8,32]{1,0:T(8,128)S(1)} %copy-done, s32[1024]{0:T(1024)S(1)} %pad_clamp_fusion), kind=kCustom, calls=%fused_computation | custom fusion | bytes 2080 | tf_op jit(solution)/shard_map/jit(_take)/gather | solution.py:91
  12.9 0.6 %fusion = f32[8,64,64]{1,2,0:T(8,128)S(1)} fusion(s32[8,32]{1,0:T(8,128)S(1)} %get-tuple-element.45, s32[8,32]{1,0:T(8,128)S(1)} %get-tuple-element.44, bf16[8,32]{1,0:T(8,128)(2,1)S(1)} %select_convert_fusion, bf16[64,64]{1,0:T(8,128)(2,1)S(1)} %convert_element_type.42), kind=kOutput, calls=%fused_computation.7 | convolution fusion | flops 6373376 | bytes 141824 | tf_op jit(solution)/shard_map/cij,jb->cib/dot_general | solution.py:35
  13.5 0.3 convolution_bitcast_fusion
  13.8 0.7 %bitcast_select_fusion = s32[8,1,32]{2,0,1:T(8,128)} fusion(s32[8,32]{1,0:T(8,128)S(1)} %gather_fusion, pred[8]{0:T(512)(128)(4,1)S(1)} %compare_and_fusion), kind=kLoop, calls=%fused_computation.40 | loop fusion | flops 256 | bytes 2056 | tf_op jit(solution)/shard_map/jit(_take)/select_n | solution.py:91
  14.4 0.1 copy.23
  14.6 0.1 reshape.322
  14.7 2.3 %all-to-all-done.1 = bf16[8,1,32]{2,1,0:T(2,128)(2,1)S(1)} async-done(((bf16[8,1,32]{2,1,0:T(2,128)(2,1)}), bf16[8,1,32]{2,1,0:T(2,128)(2,1)S(1)}, u32[]{:S(2)}, u32[]{:S(2)}) %all-to-all-start.1) | async-done | bytes 544 | tf_op jit(solution)/shard_map/all_to_all | solution.py:95
  16.9 3.3 %all-to-all-start = ((s32[8,1,32]{2,1,0:T(1,128)}), s32[8,1,32]{2,1,0:T(1,128)S(1)}, u32[]{:S(2)}, u32[]{:S(2)}) async-start(s32[8,1,32]{2,1,0:T(1,128)} %bitcast.1), calls=%async_computation | async-start | bytes 8192 | tf_op jit(solution)/shard_map/all_to_all | solution.py:96
  20.3 0.6 %subtract_convert_fusion = bf16[8,4096]{1,0:T(8,128)(2,1)} fusion(f32[8,4096]{1,0:T(8,128)S(1)} %reshape.322, bf16[8,4096]{1,0:T(8,128)(2,1)S(1)} %copy-done.1), kind=kLoop, calls=%fused_computation.10 | loop fusion | flops 98304 | bytes 262144 | tf_op jit(solution)/shard_map/convert_element_type | solution.py:89
  20.9 0.1 broadcast_in_dim.103
  21.0 3.8 %all-to-all-done = s32[8,1,32]{2,1,0:T(1,128)S(1)} async-done(((s32[8,1,32]{2,1,0:T(1,128)}), s32[8,1,32]{2,1,0:T(1,128)S(1)}, u32[]{:S(2)}, u32[]{:S(2)}) %all-to-all-start) | async-done | bytes 1056 | tf_op jit(solution)/shard_map/all_to_all | solution.py:96
  24.8 0.5 broadcast.298
  25.3 0.7 %reduce.6 = s32[8,32]{1,0:T(8,128)S(1)} reduce(s32[8,1,32]{2,1,0:T(1,128)S(1)} %all-to-all-done, s32[]{:T(128)} %broadcast.298), dimensions={1}, to_apply=%all_to_all.4.reduce_sub_computation.3 | reduce | bytes 2052 | tf_op jit(solution)/shard_map/all_to_all | solution.py:96
  26.0 0.1 squeeze.13
  26.1 0.1 fusion.10
  26.2 19.4 %psum.7 = f32[64,64]{1,0:T(8,128)S(1)} all-reduce(f32[64,64]{1,0:T(8,128)S(1)} %fusion.10), channel_id=1, replica_groups=mesh['grp'=8,'rep'=4] {'rep'}, use_global_device_ids=true, to_apply=%region_0.0 | all-reduce | flops 4096 | bytes 32768 | tf_op jit(solution)/shard_map/psum | solution.py:99
  45.6 0.1 fusion.29
  45.7 0.2 fusion.1
  46.0 0.1 copy.21
  46.1 0.1 reshape.353
  46.2 8.3 %all-gather = bf16[8,1,4096]{2,1,0:T(2,128)(2,1)S(1)} all-gather(bf16[1,1,4096]{2,1,0:T(2,128)(2,1)S(1)} %reshape.353), channel_id=1, replica_groups=mesh['grp'=8,'rep'=4] {'grp'}, dimensions={0}, use_global_device_ids=true | all-gather | bytes 73728 | tf_op jit(solution)/shard_map/all_gather | solution.py:101
  54.4 0.7 %copy.27 = bf16[8,1,4096]{2,0,1:T(8,128)(2,1)} copy(bf16[8,1,4096]{2,1,0:T(2,128)(2,1)S(1)} %all-gather) | data formatting | bytes 131072
  (11 shorter events, 0.1 us)
Async XLA Ops:
  0.6 0.7 %copy-start.2 = (s32[8]{0:T(128)S(1)}, s32[8]{0:T(128)}, u32[]{:S(2)}) copy-start(s32[8]{0:T(128)} %param.7) | copy-start | bytes 100
  1.4 0.7 %copy-start = (s32[8,32]{1,0:T(8,128)S(1)}, s32[8,32]{1,0:T(8,128)}, u32[]{:S(2)}) copy-start(s32[8,32]{1,0:T(8,128)} %param.6) | copy-start | bytes 3076
  1.4 1.0 %copy-start.1 = (bf16[8,4096]{1,0:T(8,128)(2,1)S(1)}, bf16[8,4096]{1,0:T(8,128)(2,1)}, u32[]{:S(2)}) copy-start(bf16[8,4096]{1,0:T(8,128)(2,1)} %param.5) | copy-start | bytes 196612
  7.1 9.8 %all-to-all-start.1 = ((bf16[8,1,32]{2,1,0:T(2,128)(2,1)}), bf16[8,1,32]{2,1,0:T(2,128)(2,1)S(1)}, u32[]{:S(2)}, u32[]{:S(2)}) async-start(bf16[8,1,32]{2,1,0:T(2,128)(2,1)} %copy.20), calls=%async_computation.1 | async-start | bytes 8192 | tf_op jit(solution)/shard_map/all_to_all | solution.py:95
  16.9 7.9 %all-to-all-start = ((s32[8,1,32]{2,1,0:T(1,128)}), s32[8,1,32]{2,1,0:T(1,128)S(1)}, u32[]{:S(2)}, u32[]{:S(2)}) async-start(s32[8,1,32]{2,1,0:T(1,128)} %bitcast.1), calls=%async_computation | async-start | bytes 8192 | tf_op jit(solution)/shard_map/all_to_all | solution.py:96
where the time goes:
time: 55.4 us; the launch traced here: 55.1 us
  blocking collectives  27.6 us (50%)
  starting transfers between devices  8.52 us (15%)
  local copies, waits for them, and re-layouts  7.25 us (13%)
  waiting for transfers between devices  6.04 us (11%)
  other arithmetic  3 us (5%)
  matrix products  1.86 us (3%)
  between operations  0.8 us (1%)
    psum x1, blocking collectives, local(): partial_sum = lax.psum(partial_sum, 'rep')  19.4 us
    all_gather x1, blocking collectives, local(): update = lax.all_gather(my_share, 'grp', axis=0, tiled=True)  8.26 us
    all_to_all x1, starting transfers between devices, local(): lax.all_to_all(shaped[0], 'grp', split_axis=0, concat_axis=2, tiled=True)  5.21 us
    all_to_all x1, waiting for transfers between devices, local(): lax.all_to_all(shaped[1], 'grp', split_axis=0, concat_axis=2, tiled=True)  3.79 us
    all_to_all x1, starting transfers between devices, local(): lax.all_to_all(shaped[1], 'grp', split_axis=0, concat_axis=2, tiled=True)  3.31 us
    gather x3, local copies, waits for them, and re-layouts, local(): jnp.take_along_axis(transform_coefficients, picked, axis=1)  2.56 us
    all_to_all x1, waiting for transfers between devices, local(): lax.all_to_all(shaped[0], 'grp', split_axis=0, concat_axis=2, tiled=True)  2.26 us
    unnamed x8, local copies, waits for them, and re-layouts  1.44 us
  transfers between devices with their start and end apart: 2, of which 2 were waited for; matrix products, arithmetic and copies ran while one was open for 6% of the time, Pallas kernels for 0%

commit v1 on v0

--- a/solution.py
+++ b/solution.py
@@ -96,7 +96,8 @@
             lax.all_to_all(shaped[1], "grp", split_axis=0, concat_axis=2, tiled=True),
         )
     )
-    partial_sum = lax.psum(partial_sum, "rep")
+    parts = lax.all_gather(partial_sum, "rep", axis=0, tiled=False)
+    partial_sum = parts.sum(axis=0)
     my_share = decode(partial_sum, cosines).astype(jnp.bfloat16)
     update = lax.all_gather(my_share, "grp", axis=0, tiled=True)
     return (update, residual_momentum)

time: 55.4 us -> 49.7 us (0.90)
  blocking collectives: 27.6 us -> 21.7 us
    psum x1 -> x0, blocking collectives: 19.4 us -> none  [local(): partial_sum = lax.psum(partial_sum, 'rep')]
    all_gather x0 -> x1, blocking collectives: none -> 13.4 us  [local(): parts = lax.all_gather(partial_sum, 'rep', axis=0, tiled=False)]
where the time goes in v1:
time: 49.7 us; the launch traced here: 49.4 us
  blocking collectives  21.7 us (44%)
  starting transfers between devices  8.52 us (17%)
  local copies, waits for them, and re-layouts  7.42 us (15%)
  waiting for transfers between devices  6.04 us (12%)
  other arithmetic  3.06 us (6%)
  matrix products  1.87 us (4%)
  between operations  0.8 us (2%)
    all_gather x1, blocking collectives, local(): parts = lax.all_gather(partial_sum, 'rep', axis=0, tiled=False)  13.4 us
    all_gather x1, blocking collectives, local(): update = lax.all_gather(my_share, 'grp', axis=0, tiled=True)  8.26 us
    all_to_all x1, starting transfers between devices, local(): lax.all_to_all(shaped[0], 'grp', split_axis=0, concat_axis=2, tiled=True)  5.21 us
    all_to_all x1, waiting for transfers between devices, local(): lax.all_to_all(shaped[1], 'grp', split_axis=0, concat_axis=2, tiled=True)  3.79 us
    all_to_all x1, starting transfers between devices, local(): lax.all_to_all(shaped[1], 'grp', split_axis=0, concat_axis=2, tiled=True)  3.31 us
    gather x3, local copies, waits for them, and re-layouts, local(): jnp.take_along_axis(transform_coefficients, picked, axis=1)  2.56 us
    all_to_all x1, waiting for transfers between devices, local(): lax.all_to_all(shaped[0], 'grp', split_axis=0, concat_axis=2, tiled=True)  2.26 us
    unnamed x8, local copies, waits for them, and re-layouts  1.44 us
  transfers between devices with their start and end apart: 2, of which 2 were waited for; matrix products, arithmetic and copies ran while one was open for 6% of the time, Pallas kernels for 0%

profile of v1, /device:TPU:0, one launch (start us, length us, event | category | flops | bytes accessed | tf_op | source)
XLA Modules:
  0.0 49.4 jit_solution(2553000437007644842)
XLA Ops:
  0.6 0.0 copy-start.2
  0.6 0.7 %compare_and_fusion = pred[8]{0:T(512)(128)(4,1)S(1)} fusion(s32[8]{0:T(128)} %param.7), kind=kLoop, calls=%fused_computation.49 | loop fusion | flops 48 | bytes 40 | tf_op jit(solution)/shard_map/jit(_take)/and | solution.py:90
  1.4 0.0 copy-done.2
  1.4 0.0 copy-start
  1.4 0.0 copy-start.1
  1.4 0.6 %copy-done = s32[8,32]{1,0:T(8,128)S(1)} copy-done((s32[8,32]{1,0:T(8,128)S(1)}, s32[8,32]{1,0:T(8,128)}, u32[]{:S(2)}) %copy-start) | copy-done | bytes 1048
  2.1 0.1 reshape.336
  2.1 0.1 cosine_multiply_fusion
  2.3 0.0 copy-done.1
  2.4 0.2 reshape.315
  2.5 0.3 convolution_bitcast_fusion.2
  2.8 0.3 convolution_bitcast_fusion.1
  3.1 0.1 copy.19
  3.2 0.2 reshape.316
  3.4 2.4 %gather_fusion.2 = bf16[256]{0:T(256)(128)(2,1)S(1)} fusion(bf16[8,4096]{1,0:T(8,128)(2,1)S(1)} %reshape.316, s32[256]{0:T(256)S(1)} %reshape.336), kind=kCustom, calls=%fused_computation.2 | custom fusion | bytes 3072 | tf_op jit(solution)/shard_map/jit(take_along_axis)/gather | solution.py:85
  5.8 0.1 reshape.339
  5.9 0.6 %gather_fusion.1 = bf16[8,32]{1,0:T(8,128)(2,1)S(1)} fusion(bf16[8,32]{1,0:T(8,128)(2,1)S(1)} %select_convert_fusion, s32[1024]{0:T(1024)S(1)} %pad_clamp_fusion), kind=kCustom, calls=%fused_computation.1 | custom fusion | bytes 1056 | tf_op jit(solution)/shard_map/jit(_take)/gather | solution.py:90
  6.4 0.1 bitcast_select_fusion.1
  6.5 0.6 %copy.20 = bf16[8,1,32]{2,1,0:T(2,128)(2,1)} copy(bf16[8,1,32]{2,0,1:T(8,128)(2,1)S(1)} %bitcast_select_fusion.1) | data formatting | bytes 1024 | tf_op jit(solution)/shard_map/jit(_take)/select_n | solution.py:90
  7.1 5.2 %all-to-all-start.1 = ((bf16[8,1,32]{2,1,0:T(2,128)(2,1)}), bf16[8,1,32]{2,1,0:T(2,128)(2,1)S(1)}, u32[]{:S(2)}, u32[]{:S(2)}) async-start(bf16[8,1,32]{2,1,0:T(2,128)(2,1)} %copy.20), calls=%async_computation.1 | async-start | bytes 8192 | tf_op jit(solution)/shard_map/all_to_all | solution.py:95
  12.3 0.6 %gather_fusion = s32[8,32]{1,0:T(8,128)S(1)} fusion(s32[8,32]{1,0:T(8,128)S(1)} %copy-done, s32[1024]{0:T(1024)S(1)} %pad_clamp_fusion), kind=kCustom, calls=%fused_computation | custom fusion | bytes 2080 | tf_op jit(solution)/shard_map/jit(_take)/gather | solution.py:91
  12.9 0.6 %fusion = f32[8,64,64]{1,2,0:T(8,128)S(1)} fusion(s32[8,32]{1,0:T(8,128)S(1)} %get-tuple-element.45, s32[8,32]{1,0:T(8,128)S(1)} %get-tuple-element.44, bf16[8,32]{1,0:T(8,128)(2,1)S(1)} %select_convert_fusion, bf16[64,64]{1,0:T(8,128)(2,1)S(1)} %convert_element_type.42), kind=kOutput, calls=%fused_computation.7 | convolution fusion | flops 6373376 | bytes 141824 | tf_op jit(solution)/shard_map/cij,jb->cib/dot_general | solution.py:35
  13.5 0.3 convolution_bitcast_fusion
  13.8 0.7 %bitcast_select_fusion = s32[8,1,32]{2,0,1:T(8,128)} fusion(s32[8,32]{1,0:T(8,128)S(1)} %gather_fusion, pred[8]{0:T(512)(128)(4,1)S(1)} %compare_and_fusion), kind=kLoop, calls=%fused_computation.40 | loop fusion | flops 256 | bytes 2056 | tf_op jit(solution)/shard_map/jit(_take)/select_n | solution.py:91
  14.4 0.1 copy.23
  14.6 0.1 reshape.319
  14.7 2.3 %all-to-all-done.1 = bf16[8,1,32]{2,1,0:T(2,128)(2,1)S(1)} async-done(((bf16[8,1,32]{2,1,0:T(2,128)(2,1)}), bf16[8,1,32]{2,1,0:T(2,128)(2,1)S(1)}, u32[]{:S(2)}, u32[]{:S(2)}) %all-to-all-start.1) | async-done | bytes 544 | tf_op jit(solution)/shard_map/all_to_all | solution.py:95
  16.9 3.3 %all-to-all-start = ((s32[8,1,32]{2,1,0:T(1,128)}), s32[8,1,32]{2,1,0:T(1,128)S(1)}, u32[]{:S(2)}, u32[]{:S(2)}) async-start(s32[8,1,32]{2,1,0:T(1,128)} %bitcast.1), calls=%async_computation | async-start | bytes 8192 | tf_op jit(solution)/shard_map/all_to_all | solution.py:96
  20.3 0.6 %subtract_convert_fusion = bf16[8,4096]{1,0:T(8,128)(2,1)} fusion(f32[8,4096]{1,0:T(8,128)S(1)} %reshape.319, bf16[8,4096]{1,0:T(8,128)(2,1)S(1)} %copy-done.1), kind=kLoop, calls=%fused_computation.10 | loop fusion | flops 98304 | bytes 262144 | tf_op jit(solution)/shard_map/convert_element_type | solution.py:89
  20.9 0.1 broadcast_in_dim.105
  21.0 3.8 %all-to-all-done = s32[8,1,32]{2,1,0:T(1,128)S(1)} async-done(((s32[8,1,32]{2,1,0:T(1,128)}), s32[8,1,32]{2,1,0:T(1,128)S(1)}, u32[]{:S(2)}, u32[]{:S(2)}) %all-to-all-start) | async-done | bytes 1056 | tf_op jit(solution)/shard_map/all_to_all | solution.py:96
  24.8 0.5 %broadcast.298 = s32[]{:T(128)} broadcast(s32[]{:T(128)} %constant.140.clone.1), dimensions={} | broadcast | bytes 8 | tf_op jit(solution)/shard_map/all_to_all | solution.py:96
  25.3 0.7 %reduce.7 = s32[8,32]{1,0:T(8,128)S(1)} reduce(s32[8,1,32]{2,1,0:T(1,128)S(1)} %all-to-all-done, s32[]{:T(128)} %broadcast.298), dimensions={1}, to_apply=%all_to_all.4.reduce_sub_computation.3 | reduce | bytes 2052 | tf_op jit(solution)/shard_map/all_to_all | solution.py:96
  26.0 0.1 squeeze.13
  26.1 0.1 fusion.10
  26.2 0.1 broadcast_in_dim.108
  26.3 13.4 %all_gather.6 = f32[4,1,4096]{2,1,0:T(1,128)S(1)} all-gather(f32[1,1,4096]{2,1,0:T(1,128)S(1)} %broadcast_in_dim.108), channel_id=1, replica_groups=mesh['grp'=8,'rep'=4] {'rep'}, dimensions={0}, use_global_device_ids=true | all-gather | bytes 81920 | tf_op jit(solution)/shard_map/all_gather | solution.py:99
  39.7 0.1 reduce_sum.9
  39.8 0.1 reshape.318
  39.9 0.1 fusion.29
  40.0 0.2 fusion.1
  40.3 0.1 copy.21
  40.4 0.1 reshape.349
  40.4 8.3 %all-gather = bf16[8,1,4096]{2,1,0:T(2,128)(2,1)S(1)} all-gather(bf16[1,1,4096]{2,1,0:T(2,128)(2,1)S(1)} %reshape.349), channel_id=1, replica_groups=mesh['grp'=8,'rep'=4] {'grp'}, dimensions={0}, use_global_device_ids=true | all-gather | bytes 73728 | tf_op jit(solution)/shard_map/all_gather | solution.py:102
  48.7 0.7 %copy.27 = bf16[8,1,4096]{2,0,1:T(8,128)(2,1)} copy(bf16[8,1,4096]{2,1,0:T(2,128)(2,1)S(1)} %all-gather) | data formatting | bytes 131072
  (11 shorter events, 0.1 us)
Async XLA Ops:
  0.6 0.7 %copy-start.2 = (s32[8]{0:T(128)S(1)}, s32[8]{0:T(128)}, u32[]{:S(2)}) copy-start(s32[8]{0:T(128)} %param.7) | copy-start | bytes 100
  1.4 0.7 %copy-start = (s32[8,32]{1,0:T(8,128)S(1)}, s32[8,32]{1,0:T(8,128)}, u32[]{:S(2)}) copy-start(s32[8,32]{1,0:T(8,128)} %param.6) | copy-start | bytes 3076
  1.4 1.0 %copy-start.1 = (bf16[8,4096]{1,0:T(8,128)(2,1)S(1)}, bf16[8,4096]{1,0:T(8,128)(2,1)}, u32[]{:S(2)}) copy-start(bf16[8,4096]{1,0:T(8,128)(2,1)} %param.5) | copy-start | bytes 196612
  7.1 9.8 %all-to-all-start.1 = ((bf16[8,1,32]{2,1,0:T(2,128)(2,1)}), bf16[8,1,32]{2,1,0:T(2,128)(2,1)S(1)}, u32[]{:S(2)}, u32[]{:S(2)}) async-start(bf16[8,1,32]{2,1,0:T(2,128)(2,1)} %copy.20), calls=%async_computation.1 | async-start | bytes 8192 | tf_op jit(solution)/shard_map/all_to_all | solution.py:95
  16.9 7.9 %all-to-all-start = ((s32[8,1,32]{2,1,0:T(1,128)}), s32[8,1,32]{2,1,0:T(1,128)S(1)}, u32[]{:S(2)}, u32[]{:S(2)}) async-start(s32[8,1,32]{2,1,0:T(1,128)} %bitcast.1), calls=%async_computation | async-start | bytes 8192 | tf_op jit(solution)/shard_map/all_to_all | solution.py:96
